TPU v7x, 32 devices: a whole 2x2x4 slice. The times are simulated.
32 devices in a mesh: groups: 2 (over y), gx: 16 (over z, x, core).
Axes of the slice: x: 2, y: 2, z: 4, core: 2. Of those that a mesh axis runs over, the one named last changes fastest.
Arguments:
- features: float32 [48, 64, 96, 128], P(None, ('groups', 'gx')), parts along dimension 1, may hold values from -6 to 6
- fine_weights: bfloat16 [1536, 8, 48, 48], P('gx'), may hold values from -1.796875 to 1.796875
- middle_weights: bfloat16 [384, 4, 48, 48], P('gx'), may hold values from -3 to 3
- lift_fine: float32 [48, 48], replicated, may hold values from -0.875 to 0.875
- lift_middle: float32 [48, 48], replicated, may hold values from -0.875 to 0.875
- project_out: float32 [48, 48], replicated, may hold values from -0.875 to 0.875
Outputs:
- result: float32 [48, 64, 96, 128], P(None, ('groups', 'gx')), parts along dimension 1
There are 2 independent parts, one for each index of `groups`. A program takes and returns all parts, laid end to end along the dimension named above; an argument that names none is the same for every part. Nothing has to cross between parts.
All inputs are finite; a program needn't handle non-finite values.
Results may differ from a plain program's by a relative error of at most 0.0018.
Values sent between devices are 32-bit elements; how exact they have to be, the bound alone decides.
No kernel may reach another device: no remote copies, remote signals or barrier semaphores. Data moves between devices by JAX's collectives and lax.ppermute only.
A program may use at most 128 MiB of HBM per device.

v0:
```python
import jax
import jax.numpy as jnp
import numpy as np
from jax import lax
from jax.experimental import pallas as pl
from jax.experimental.pallas import tpu as pltpu
from jax.sharding import PartitionSpec as P

KY = 48
KZ = 32
LANES = 128
PAD = 16
GROUP = 16
HIGHEST = lax.Precision.HIGHEST
BF = jnp.bfloat16
F32 = jnp.float32
MIB = 1 << 20


def cosine(modes_kept, length):
    orders = np.arange(modes_kept)[:, None]
    points = np.arange(length)[None, :]
    phase = orders * (2 * points + 1) % (4 * length)
    scales = np.where(orders == 0, np.sqrt(1.0 / length), np.sqrt(2.0 / length))
    return scales * np.cos(np.pi / (2 * length) * phase)


def halves(table):
    table = np.asarray(table, np.float32)
    high = table.astype(BF)
    low = (table - high.astype(np.float32)).astype(BF)
    return high, low


def split(values):
    high = values.astype(BF)
    return high, (values - high.astype(F32)).astype(BF)


def dot(a, b):
    return jnp.dot(a, b, preferred_element_type=F32)


def gelu(t):
    return 0.5 * t * (1.0 + lax.erf(t * np.float32(np.sqrt(0.5))))


def vmem_call(body, outs, args, scratch, limit, hbm_out=False):
    in_vmem = pl.BlockSpec(memory_space=pltpu.VMEM)
    out_specs = tuple(
        pl.BlockSpec(memory_space=pl.ANY if hbm_out else pltpu.VMEM) for _ in outs
    )
    shapes = tuple(jax.ShapeDtypeStruct(s, F32) for s in outs)
    single = len(outs) == 1
    return pl.pallas_call(
        body,
        out_shape=shapes[0] if single else shapes,
        in_specs=[in_vmem] * len(args),
        out_specs=out_specs[0] if single else out_specs,
        scratch_shapes=scratch,
        compiler_params=pltpu.CompilerParams(vmem_limit_bytes=limit * MIB),
        name=body.__name__,
    )(*args)


def interleave_matrix(matrix, factor, transposed_rows):
    channels = matrix.shape[0]
    rows = channels * 8 * factor
    cols = channels * 8
    spread_rows = (
        lax.broadcasted_iota(jnp.int32, (channels, rows), 1) // (8 * factor)
        == lax.broadcasted_iota(jnp.int32, (channels, rows), 0)
    )
    spread_cols = (
        lax.broadcasted_iota(jnp.int32, (channels, cols), 1) // 8
        == lax.broadcasted_iota(jnp.int32, (channels, cols), 0)
    ).astype(F32).astype(BF)
    spread_rows = spread_rows.astype(F32).astype(BF)
    keep = (
        lax.broadcasted_iota(jnp.int32, (rows, cols), 0) % (8 * factor) // factor
        == lax.broadcasted_iota(jnp.int32, (rows, cols), 1) % 8
    )
    parts = []
    for part in split(matrix):
        tall = lax.dot_general(part, spread_cols, (((0,), (0,)), ((), ())), preferred_element_type=F32)
        wide = lax.dot_general(
            spread_rows, tall.astype(BF), (((0,), (0,)), ((), ())), preferred_element_type=F32
        )
        parts.append(jnp.where(keep, wide, 0.0).astype(BF))
    return parts


def forward_fine(v_ref, wz_ref, ty_ref, out_ref, z_ref):
    channels, local_x, cells_y, cells_z = v_ref.shape
    half = channels // 2
    chunk = 6
    for first in range(0, half, chunk):
        rows = [
            jnp.concatenate(
                [v_ref[c, x] for c in (cp, cp + half) for x in range(local_x)], axis=1
            )
            for cp in range(first, first + chunk)
        ]
        high, low = split(jnp.concatenate(rows, axis=0))
        wide = dot(high, wz_ref[...])
        total = wide[:, :LANES] + wide[:, LANES:] + dot(low, wz_ref[:, :LANES])
        for n in range(chunk):
            z_ref[first + n] = total[n * cells_y : (n + 1) * cells_y]
    modes_y = ty_ref.shape[0] // 2
    for cp in range(0, half, 2):
        high, low = split(jnp.concatenate([z_ref[cp], z_ref[cp + 1]], axis=1))
        both = dot(ty_ref[...], jnp.concatenate([high, low], axis=0))
        both = both[:modes_y] + both[modes_y:]
        for n in range(2):
            out_ref[pl.ds(cp + n, modes_y, stride=half), :] = both[:, n * LANES : (n + 1) * LANES]


def fine_coefficients(features):
    channels, local_x, cells_y, cells_z = features.shape
    high, low = halves(cosine(KZ, cells_z).T)
    eye = np.eye(2 * local_x, dtype=np.float32)
    wz = np.concatenate(
        [np.kron(eye, part.astype(np.float32)) for part in (high, low)], axis=1
    ).astype(BF)
    high, low = halves(cosine(KY, cells_y))
    ty = np.block([[high, high], [low, np.zeros_like(low)]]).astype(BF)
    return vmem_call(
        forward_fine,
        [(KY * channels // 2, LANES)],
        (features, jnp.asarray(wz), jnp.asarray(ty)),
        [pltpu.VMEM((channels // 2, cells_y, LANES), F32)],
        24,
    )


def mix_fine(r_ref, w_ref, tv_ref, out_ref, modal_ref, mixed_ref, spread_ref):
    members, rows, _ = r_ref.shape
    modes_x, channels, _, owned = w_ref.shape
    half = channels // 2
    per = owned // KZ
    quarter = lax.broadcasted_iota(jnp.int32, (half, LANES), 1) // KZ
    for first in range(0, modes_x, 4):
        acc = [None] * 4
        for a in range(members):
            block = r_ref[a]
            for n in range(4):
                term = block * tv_ref[(first + n) * members + a][None, :]
                acc[n] = term if a == 0 else acc[n] + term
        for n in range(4):
            both = acc[n] + pltpu.roll(acc[n], LANES - KZ, 1)
            for c2 in range(2):
                placed = None
                for i in range(per):
                    piece = both[i * half : (i + 1) * half]
                    shift = (KZ * i - 2 * KZ * c2) % LANES
                    piece = pltpu.roll(piece, shift, 1) if shift else piece
                    placed = piece if placed is None else jnp.where(quarter == i, piece, placed)
                modal_ref[first + n, c2 * half : (c2 + 1) * half, :] = placed.astype(BF).astype(F32)

    def one_mode(k, carry):
        total = None
        for c in range(channels):
            term = modal_ref[k, c : c + 1, :owned] * w_ref[k, c].astype(F32)
            total = term if total is None else total + term
        mixed_ref[k, :, :owned] = total
        return carry

    lax.fori_loop(0, modes_x, one_mode, 0)
    for k in range(modes_x):
        for i in range(per):
            placed = None
            for q in range(4):
                c2 = q // 2
                piece = mixed_ref[k, c2 * half : (c2 + 1) * half, :]
                shift = (KZ * q - KZ * i) % LANES
                piece = pltpu.roll(piece, shift, 1) if shift else piece
                placed = piece if placed is None else jnp.where(quarter == q, piece, placed)
            spread_ref[k, i * half : (i + 1) * half, :] = placed
    for a in range(members):
        total = None
        for k in range(modes_x):
            term = spread_ref[k] * tv_ref[k * members + a][None, :]
            total = term if total is None else total + term
        out_ref[a] = total


def fine_mixed(received, weights, local_x):
    members, rows, _ = received.shape
    owned, modes_x, channels, _ = weights.shape
    table = cosine(modes_x, members * local_x).reshape(modes_x * members, local_x)
    lanes = np.tile(np.repeat(table, KZ, axis=1), (1, 2)).astype(np.float32)
    return vmem_call(
        mix_fine,
        [received.shape],
        (received, jnp.transpose(weights, (1, 2, 3, 0)), jnp.asarray(lanes)),
        [
            pltpu.VMEM((modes_x, channels, LANES), F32),
            pltpu.VMEM((modes_x, channels, LANES), F32),
            pltpu.VMEM((modes_x, rows, LANES), F32),
        ],
        16,
    )


def lift_blocks(source, parts, cells_y, store):
    channels = source.shape[0]
    for y in range(0, cells_y, 16):
        block = jnp.concatenate(
            [source[:, y + s : y + s + 8, :].reshape(channels * 8, LANES) for s in (0, 8)], axis=1
        )
        high, low = split(block)
        done = dot(parts[0], high) + dot(parts[1], high) + dot(parts[0], low)
        rows = done.shape[0] // channels
        for n in range(2):
            store(y + 8 * n, done[:, n * LANES : (n + 1) * LANES].reshape(channels, rows, LANES))


def lift_fine_kernel(v_ref, a_ref, out_ref):
    parts = interleave_matrix(a_ref[...], 1, False)
    for x in range(v_ref.shape[1]):
        def store(y, value, x=x):
            out_ref[:, x, y : y + 8, :] = value
        lift_blocks(v_ref.at[:, x], parts, v_ref.shape[2], store)


def project_kernel(v_ref, a_ref, base_ref, out_ref):
    parts = interleave_matrix(a_ref[...], 1, False)
    for x in range(v_ref.shape[1]):
        def store(y, value, x=x):
            out_ref[:, x, y : y + 8, :] = value + base_ref[:, x, y : y + 8, :]
        lift_blocks(v_ref.at[:, x], parts, v_ref.shape[2], store)


def lift_coarse_kernel(v_ref, a_ref, pz_ref, out_ref, p_ref):
    parts = interleave_matrix(a_ref[...], 1, False)
    channels, cells_y, _ = v_ref.shape

    def store(y, value):
        p_ref[:, y : y + 8, :] = value

    lift_blocks(v_ref, parts, cells_y, store)
    rows = jnp.concatenate(
        [jnp.concatenate([p_ref[c], p_ref[c + 1]], axis=1) for c in range(0, channels, 2)], axis=0
    )
    high, low = split(rows)
    done = dot(high, pz_ref[...]) + dot(low, pz_ref[...])
    for cg in range(channels // GROUP):
        for t in range(GROUP // 2):
            n = cg * (GROUP // 2) + t
            out_ref[cg * cells_y : (cg + 1) * cells_y, t * LANES : (t + 1) * LANES] = done[
                n * cells_y : (n + 1) * cells_y
            ]


def inverse_fine(r_ref, lift_ref, ty_ref, bz_ref, yc_ref, ec_ref, level_ref, pool_ref, out_ref,
                 g_ref, q_ref, w_ref, d_ref, place):
    channels, local_x, cells_y, cells_z = lift_ref.shape
    half = channels // 2
    modes_y = r_ref.shape[0] // half
    half_ky = modes_y // 2
    coarse_y = cells_y // 2
    for cp in range(0, half, 2):
        block = jnp.concatenate(
            [r_ref[pl.ds(cp + n, modes_y, stride=half), :] for n in range(2)], axis=1
        )
        high, low = split(block)
        both = dot(ty_ref[...], jnp.concatenate([high, low, high], axis=0)).astype(BF)
        for n in range(2):
            part = both[:, n * LANES : (n + 1) * LANES]
            g_ref[(cp + n) * cells_y : (cp + n + 1) * cells_y, :] = jnp.concatenate(
                [part, part], axis=1
            )
    lane = lax.broadcasted_iota(jnp.int32, (cells_z, 2 * LANES), 1) % GROUP
    for c in range(GROUP):
        for part in range(2):
            w_ref[part, c * cells_z : (c + 1) * cells_z, :] = jnp.where(
                lane == c, ec_ref[part].astype(F32), 0.0
            ).astype(BF)
    chunk = 4
    for first in range(0, half, chunk):
        wide = dot(g_ref[first * cells_y : (first + chunk) * cells_y, :], bz_ref[...])
        for n in range(chunk):
            cp = first + n
            tall = []
            for c2 in range(2):
                column = []
                for x in range(local_x):
                    q = c2 * local_x + x
                    piece = wide[n * cells_y : (n + 1) * cells_y, q * LANES : (q + 1) * LANES]
                    piece = gelu(piece + lift_ref[cp + c2 * half, x])
                    level_ref[cp + c2 * half, x] = piece
                    column.append(piece.astype(BF))
                tall.append(jnp.concatenate(column, axis=0))
            down = dot(yc_ref[...], jnp.concatenate(tall, axis=1))
            for c2 in range(2):
                c = cp + c2 * half
                cg, inner = c // GROUP, c % GROUP
                part = down[:, c2 * LANES : (c2 + 1) * LANES]
                q_ref[cg * half_ky : (cg + 1) * half_ky, inner * LANES : (inner + 1) * LANES] = (
                    part[:half_ky] + part[half_ky : 2 * half_ky]
                )
                pool_ref[c] = part[2 * half_ky :]
    high, low = split(q_ref[...])
    d_ref[...] = dot(high, w_ref[0]) + dot(low, w_ref[0]) + dot(high, w_ref[1])
    out_ref[...] = jnp.zeros_like(out_ref)
    for (cg, jh, i), row in place.items():
        source = cg * half_ky + i
        out_ref[row : row + 1, :] = d_ref[source : source + 1, jh * LANES : (jh + 1) * LANES]


def fine_level(received, lifted, place, place_rows):
    channels, local_x, cells_y, cells_z = lifted.shape
    half_ky, half_kz = KY // 2, KZ // 2
    coarse_y, coarse_z = cells_y // 2, cells_z // 2
    high, low = halves(cosine(KY, cells_y).T)
    ty = np.concatenate([high, high, low], axis=1)
    eye = np.eye(2 * local_x, dtype=np.float32)
    bz = np.concatenate(
        [np.kron(eye, part.astype(np.float32)) for part in halves(cosine(KZ, cells_z))], axis=0
    ).astype(BF)
    pool_y = np.kron(np.eye(coarse_y), np.ones((1, 2))) / (2.0 * local_x)
    pool_z = np.kron(np.eye(coarse_z), np.ones((1, 2))) / 2.0
    high, low = halves(cosine(half_ky, coarse_y) @ pool_y)
    yc = np.concatenate([high, low, pool_y.astype(BF)], axis=0)
    yc = np.concatenate([yc] * local_x, axis=1)
    ec = np.repeat((cosine(half_kz, coarse_z) @ pool_z).T, GROUP, axis=1)
    ec = np.stack(halves(ec))
    groups = channels // GROUP

    def inverse_fine_kernel(*refs):
        inverse_fine(*refs, place)

    return vmem_call(
        inverse_fine_kernel,
        [lifted.shape, (channels, coarse_y, cells_z), (place_rows, LANES)],
        (received, lifted, jnp.asarray(ty), jnp.asarray(bz), jnp.asarray(yc), jnp.asarray(ec)),
        [
            pltpu.VMEM((channels // 2 * cells_y, 2 * LANES), BF),
            pltpu.VMEM((groups * half_ky, GROUP * cells_z), F32),
            pltpu.VMEM((2, GROUP * cells_z, 2 * LANES), BF),
            pltpu.VMEM((groups * half_ky, 2 * LANES), F32),
        ],
        28,
    )


def mix_coarse(r_ref, w_ref, out_ref, table, rows):
    members, pad, _ = r_ref.shape
    owned, modes_x, channels, _ = w_ref.shape
    groups = channels // GROUP
    inner = LANES // GROUP
    units = owned // inner
    lane = lax.broadcasted_iota(jnp.int32, (rows, LANES), 1)
    row = lax.broadcasted_iota(jnp.int32, (rows, channels), 0)
    modal = []
    for k in range(modes_x):
        total = None
        for a in range(members):
            term = r_ref[a] * float(table[k, a])
            total = term if total is None else total + term
        modal.append(total)
    fill = jnp.zeros((rows - modes_x * units, LANES), F32)
    packed = [
        jnp.concatenate(
            [modal[k][cg * units : (cg + 1) * units] for k in range(modes_x)] + [fill], axis=0
        )
        for cg in range(groups)
    ]
    mixed = []
    for j in range(inner):
        placed = None
        for cg in range(groups):
            shift = (GROUP * cg - GROUP * j) % LANES
            piece = pltpu.roll(packed[cg], shift, 1) if shift else packed[cg]
            placed = piece if placed is None else jnp.where(lane // GROUP == cg, piece, placed)
        left = placed[:, :channels].astype(BF)
        total = jnp.zeros((rows, channels), F32)
        for k in range(modes_x):
            for u in range(units):
                full = dot(left, w_ref[u * inner + j, k])
                total = jnp.where(row == k * units + u, full, total)
        mixed.append(jnp.concatenate([total, jnp.zeros((rows, LANES - channels), F32)], axis=1))
    spread = []
    for cg in range(groups):
        placed = None
        for j in range(inner):
            shift = (GROUP * j - GROUP * cg) % LANES
            piece = pltpu.roll(mixed[j], shift, 1) if shift else mixed[j]
            placed = piece if placed is None else jnp.where(lane // GROUP == j, piece, placed)
        spread.append(placed)
    final = []
    for k in range(modes_x):
        final.append(
            jnp.concatenate(
                [spread[cg][k * units : (k + 1) * units] for cg in range(groups)]
                + [jnp.zeros((pad - groups * units, LANES), F32)],
                axis=0,
            )
        )
    for a in range(members):
        total = None
        for k in range(modes_x):
            term = final[k] * float(table[k, a])
            total = term if total is None else total + term
        out_ref[a] = total


def coarse_mixed(received, weights, coarse_x):
    owned, modes_x, channels, _ = weights.shape
    table = cosine(modes_x, coarse_x)
    units = owned * GROUP // LANES
    rows = -(-modes_x * units // 16) * 16

    def mix_coarse_kernel(*refs):
        mix_coarse(*refs, table, rows)

    return vmem_call(mix_coarse_kernel, [received.shape], (received, weights), [], 16)


def finish(r_ref, lift_ref, base_ref, a_ref, yi_ref, ei_ref, up_ref, out_ref, b_ref, l_ref, res_ref, sems):
    channels, local_x, cells_y, cells_z = base_ref.shape
    coarse_y = cells_y // 2
    groups = channels // GROUP
    coarse_z = cells_z // 2
    lane = lax.broadcasted_iota(jnp.int32, (2 * LANES, LANES), 1) // coarse_z
    row = lax.broadcasted_iota(jnp.int32, (2 * LANES, LANES), 0) % GROUP
    for t in range(GROUP // 2):
        for part in range(2):
            b_ref[part, :, t * LANES : (t + 1) * LANES] = jnp.where(
                row == 2 * t + lane, ei_ref[part].astype(F32), 0.0
            ).astype(BF)
    high, low = split(r_ref[...])
    grid = dot(yi_ref[0], high) + dot(yi_ref[0], low) + dot(yi_ref[1], high)
    left = jnp.concatenate(
        [
            jnp.concatenate(
                [grid[(2 * cg + jh) * coarse_y : (2 * cg + jh + 1) * coarse_y] for jh in range(2)],
                axis=1,
            )
            for cg in range(groups)
        ],
        axis=0,
    )
    high, low = split(left)
    level = dot(high, b_ref[0]) + dot(low, b_ref[0]) + dot(high, b_ref[1])
    level = gelu(level + lift_ref[...])
    for cg in range(groups):
        tall = jnp.concatenate(
            [
                level[cg * coarse_y : (cg + 1) * coarse_y, t * LANES : (t + 1) * LANES]
                for t in range(GROUP // 2)
            ],
            axis=0,
        )
        high, low = split(tall)
        wide = dot(jnp.concatenate([high, low], axis=1), up_ref[...])
        for t in range(GROUP // 2):
            for c2 in range(2):
                l_ref[cg * GROUP + 2 * t + c2] = wide[
                    t * coarse_y : (t + 1) * coarse_y, c2 * LANES : (c2 + 1) * LANES
                ]
    parts = interleave_matrix(a_ref[...], 2, False)
    copies = []

    def store(y, value):
        for x in range(local_x):
            res_ref[:, x, 2 * y : 2 * y + 16, :] = value + base_ref[:, x, 2 * y : 2 * y + 16, :]
        if y % 16 == 8:
            span = pl.ds(2 * y - 16, 32)
            copy = pltpu.make_async_copy(
                res_ref.at[:, :, span, :], out_ref.at[:, :, span, :], sems.at[y // 16]
            )
            copy.start()
            copies.append(copy)

    lift_blocks(l_ref, parts, coarse_y, store)
    for copy in copies:
        copy.wait()


def final_result(received, lifted, base, matrix, place, place_rows):
    channels, local_x, cells_y, cells_z = base.shape
    half_ky, half_kz = KY // 2, KZ // 2
    coarse_y, coarse_z = cells_y // 2, cells_z // 2
    groups = channels // GROUP
    table_y = cosine(half_ky, coarse_y)
    left = np.zeros((groups, 2, coarse_y, place_rows))
    for (cg, jh, i), row in place.items():
        left[cg, jh, :, row] = table_y[i]
    yi = np.stack(halves(left.reshape(groups * 2 * coarse_y, place_rows)))
    inverse_z = np.repeat(cosine(half_kz, coarse_z), GROUP, axis=0)
    ei = np.stack(halves(np.concatenate([inverse_z] * (LANES // coarse_z), axis=1)))
    up = np.kron(np.eye(2), np.kron(np.eye(coarse_z), np.ones((1, 2))))
    up = np.concatenate([up, up], axis=0).astype(BF)
    args = (received, lifted, base, matrix, jnp.asarray(yi), jnp.asarray(ei), jnp.asarray(up))
    return vmem_call(
        finish,
        [base.shape],
        args,
        [
            pltpu.VMEM((2, 2 * LANES, GROUP // 2 * LANES), BF),
            pltpu.VMEM((channels, coarse_y, cells_z), F32),
            pltpu.VMEM(base.shape, F32),
            pltpu.SemaphoreType.DMA((coarse_y // 16,)),
        ],
        32,
        hbm_out=True,
    )


def swap(blocks):
    return lax.all_to_all(blocks, "gx", split_axis=0, concat_axis=0, tiled=True)


def plain_mix(coeffs, weights, cells_x):
    group_size = lax.axis_size("gx")
    table_x = jnp.asarray(cosine(weights.shape[1], cells_x), F32)
    pencils = lax.all_to_all(coeffs, "gx", split_axis=0, concat_axis=1, tiled=True)
    modal = jnp.einsum("mxc,kx->mkc", pencils, table_x, precision=HIGHEST)
    mixed = jnp.einsum(
        "mkc,mkco->mko", modal.astype(BF), weights, preferred_element_type=F32
    )
    back = jnp.einsum("mkc,kx->mxc", mixed, table_x, precision=HIGHEST)
    return lax.all_to_all(back, "gx", split_axis=1, concat_axis=0, tiled=True)


def on_device(features, fine_weights, middle_weights, lift_fine, lift_middle, project_out):
    channels, local_x, cells_y, cells_z = features.shape
    group_size = lax.axis_size("gx")
    cells_x = local_x * group_size
    half = channels // 2
    half_ky, half_kz = KY // 2, KZ // 2
    groups = channels // GROUP
    inner = LANES // GROUP

    coeffs = fine_coefficients(features)
    owned = fine_weights.shape[0]
    if owned % KZ == 0 and owned <= LANES:
        received = swap(coeffs.reshape(group_size, -1, LANES))
        mixed = fine_mixed(received, fine_weights, local_x)
        slabs = swap(mixed).reshape(coeffs.shape)
    else:
        modes = coeffs.reshape(KY, half, 2, local_x, KZ).transpose(0, 4, 3, 2, 1)
        slabs = plain_mix(modes.reshape(KY * KZ, local_x, channels), fine_weights, cells_x)
        slabs = slabs.reshape(KY, KZ, local_x, 2, half).transpose(0, 4, 3, 2, 1)
        slabs = slabs.reshape(coeffs.shape)
    lifted = vmem_call(lift_fine_kernel, [features.shape], (features, lift_fine), [], 24)

    owned = middle_weights.shape[0]
    direct = owned % inner == 0 and groups * (owned // inner) <= PAD
    place = {}
    for cg in range(groups):
        for i in range(half_ky):
            for jh in range(2):
                if direct:
                    member, unit = divmod(2 * i + jh, owned // inner)
                    place[cg, jh, i] = member * PAD + cg * (owned // inner) + unit
                else:
                    place[cg, jh, i] = (jh * groups + cg) * half_ky + i
    place_rows = group_size * PAD if direct else 2 * groups * half_ky
    level_one, pool_y, coarse = fine_level(slabs, lifted, place, place_rows)
    base = vmem_call(project_kernel, [features.shape], (level_one, project_out, features), [], 28)
    pool_z = np.kron(np.eye(cells_z // 2), np.ones((1, 2))).T / 2.0
    pool_z = jnp.asarray(np.kron(np.eye(2), pool_z).astype(BF))
    coarse_lift = vmem_call(
        lift_coarse_kernel,
        [(groups * cells_y // 2, GROUP // 2 * LANES)],
        (pool_y, lift_middle, pool_z),
        [pltpu.VMEM(pool_y.shape, F32)],
        16,
    )
    coarse_x = cells_x // 2
    if direct:
        received = swap(coarse.reshape(group_size, PAD, LANES))
        mixed = coarse_mixed(received, middle_weights, coarse_x)
        slabs = swap(mixed).reshape(coarse.shape)
    else:
        modes = coarse.reshape(2, groups, half_ky, inner, GROUP).transpose(2, 0, 3, 1, 4)
        slabs = plain_mix(
            modes.reshape(half_ky * half_kz, 1, channels), middle_weights, coarse_x
        )
        slabs = slabs.reshape(half_ky, 2, inner, groups, GROUP).transpose(1, 3, 0, 2, 4)
        slabs = slabs.reshape(coarse.shape)
    return final_result(slabs, coarse_lift, base, project_out, place, place_rows)


def solution(mesh):
    in_specs = (
        P(None, ("groups", "gx"), None, None),
        P("gx", None, None, None),
        P("gx", None, None, None),
        P(),
        P(),
        P(),
    )
    out_specs = P(None, ("groups", "gx"), None, None)
    return jax.shard_map(
        on_device, mesh=mesh, in_specs=in_specs, out_specs=out_specs, check_vma=False
    )
```

profile of v0, /device:TPU:0, one launch (start us, length us, event | category | flops | bytes accessed | tf_op | source)
XLA Modules:
  0.0 98.5 jit_solution(14555393284585691680)
XLA Ops:
  0.0 2.3 %copy-done = f32[48,2,96,128]{3,2,1,0:T(8,128)S(1)} copy-done((f32[48,2,96,128]{3,2,1,0:T(8,128)S(1)}, f32[48,2,96,128]{3,2,1,0:T(8,128)}, u32[]{:S(2)}) %copy-start) | copy-done | bytes 4718616
  2.3 0.9 copy-done.13
  3.3 0.8 copy-done.22
  4.1 1.6 %forward_fine.1 = f32[1152,128]{1,0:T(8,128)S(1)} custom-call(f32[48,2,96,128]{3,2,1,0:T(8,128)S(1)} %copy-done, bf16[512,256]{1,0:T(8,128)(2,1)S(1)} %copy-done.13, bf16[96,192]{1,0:T(8,128)(2,1)S(1)} %copy-done.22), custom_call_target="tpu_custom_call" | custom-call | tf_op jit(solution)/shard_map/forward_fine/pallas_call | solution.py:55
  5.7 0.0 copy-start.24
  5.7 24.4 %all_to_all.20.r_ref = f32[16,72,128]{2,1,0:T(8,128)S(1)} all-to-all(f32[16,72,128]{2,1,0:T(8,128)S(1)} %bitcast.7), channel_id=1, replica_groups=mesh['groups'=2,'gx'=16] {'gx'}, dimensions={0} | all-to-all | bytes 1179648 | tf_op jit(solution)/shard_map/all_to_all | solution.py:512
  30.1 0.0 copy-done.7
  30.1 0.0 copy-done.18
  30.1 3.0 %mix_fine.1 = f32[16,72,128]{2,1,0:T(8,128)} custom-call(f32[16,72,128]{2,1,0:T(8,128)S(1)} %all_to_all.20.r_ref, bf16[8,48,48,96]{3,2,1,0:T(8,128)(2,1)S(1)} %bitcast.5, f32[128,128]{1,0:T(8,128)S(1)} %copy-done.18), custom_call_target="tpu_custom_call" | custom-call | tf_op jit(solution)/shard_map/mix_fine/pallas_call | solution.py:55
  33.0 3.6 %all-to-all-start.1 = ((f32[16,72,128]{2,1,0:T(8,128)}), f32[16,72,128]{2,1,0:T(8,128)S(1)}, u32[]{:S(2)}, u32[]{:S(2)}) async-start(f32[16,72,128]{2,1,0:T(8,128)} %mix_fine.1), calls=%async_computation.1 | async-start | bytes 1179648 | tf_op jit(solution)/shard_map/all_to_all | solution.py:512
  36.6 0.0 copy-done.24
  36.6 0.0 copy-start.1
  36.7 2.3 %copy-done.1 = f32[48,2,96,128]{3,2,1,0:T(8,128)S(1)} copy-done((f32[48,2,96,128]{3,2,1,0:T(8,128)S(1)}, f32[48,2,96,128]{3,2,1,0:T(8,128)}, u32[]{:S(2)}) %copy-start.1) | copy-done | bytes 4718616
  39.0 0.0 copy-start.10
  39.0 0.0 copy-start.17
  39.0 4.3 %lift_fine_kernel.1.refs_1_ = f32[48,2,96,128]{3,2,1,0:T(8,128)S(1)} custom-call(f32[48,2,96,128]{3,2,1,0:T(8,128)S(1)} %copy-done.1, f32[48,48]{1,0:T(8,128)S(1)} %copy-done.24), custom_call_target="tpu_custom_call" | custom-call | tf_op jit(solution)/shard_map/lift_fine_kernel/pallas_call | solution.py:55
  43.3 0.0 copy-start.3
  43.3 2.2 %copy-done.3 = f32[48,2,96,128]{3,2,1,0:T(8,128)} copy-done((f32[48,2,96,128]{3,2,1,0:T(8,128)}, f32[48,2,96,128]{3,2,1,0:T(8,128)S(1)}, u32[]{:S(2)}) %copy-start.3) | copy-done | bytes 4718616
  45.5 6.6 %all-to-all-done.1 = f32[16,72,128]{2,1,0:T(8,128)S(1)} async-done(((f32[16,72,128]{2,1,0:T(8,128)}), f32[16,72,128]{2,1,0:T(8,128)S(1)}, u32[]{:S(2)}, u32[]{:S(2)}) %all-to-all-start.1) | async-done | bytes 589856 | tf_op jit(solution)/shard_map/all_to_all | solution.py:512
  52.1 0.0 copy-done.12
  52.1 0.0 copy-done.16
  52.1 0.0 copy-done.20
  52.1 0.0 copy-done.21
  52.1 0.0 copy-start.4
  52.1 2.3 %copy-done.4 = f32[48,2,96,128]{3,2,1,0:T(8,128)S(1)} copy-done((f32[48,2,96,128]{3,2,1,0:T(8,128)S(1)}, f32[48,2,96,128]{3,2,1,0:T(8,128)}, u32[]{:S(2)}) %copy-start.4) | copy-done | bytes 4718616
  54.5 3.3 %inverse_fine_kernel.1 = (f32[48,2,96,128]{3,2,1,0:T(8,128)S(1)}, f32[48,48,128]{2,1,0:T(8,128)S(1)}, f32[256,128]{1,0:T(8,128)S(1)}) custom-call(f32[1152,128]{1,0:T(8,128)S(1)} %bitcast.6, f32[48,2,96,128]{3,2,1,0:T(8,128)S(1)} %copy-done.4, bf16[96,144]{1,0:T(8,128)(2,1)S(1)} %copy-done.21, bf16[256,512]{1,0:T(8,128)(2,1)S(1)} %copy-done.12, ...), custom_call_target="tpu_custom_call" | custom-call | tf_op jit(solution)/shard_map/inverse_fine_kernel/pallas_call | solution.py:55
  57.8 0.0 copy-start.8
  57.8 2.2 %copy-done.8 = f32[48,2,96,128]{3,2,1,0:T(8,128)} copy-done((f32[48,2,96,128]{3,2,1,0:T(8,128)}, f32[48,2,96,128]{3,2,1,0:T(8,128)S(1)}, u32[]{:S(2)}) %copy-start.8) | copy-done | bytes 4718616
  60.0 12.0 %all_to_all.21.refs_0_ = f32[16,16,128]{2,1,0:T(8,128)S(1)} all-to-all(f32[16,16,128]{2,1,0:T(8,128)S(1)} %bitcast.9), channel_id=1, replica_groups=mesh['groups'=2,'gx'=16] {'gx'}, dimensions={0} | all-to-all | bytes 262144 | tf_op jit(solution)/shard_map/all_to_all | solution.py:512
  72.0 0.0 copy-done.10
  72.0 1.3 %mix_coarse_kernel.1 = f32[16,16,128]{2,1,0:T(8,128)} custom-call(f32[16,16,128]{2,1,0:T(8,128)S(1)} %all_to_all.21.refs_0_, bf16[24,4,48,48]{3,2,1,0:T(8,128)(2,1)S(1)} %copy-done.10), custom_call_target="tpu_custom_call" | custom-call | tf_op jit(solution)/shard_map/mix_coarse_kernel/pallas_call | solution.py:55
  73.3 3.7 %all-to-all-start.3 = ((f32[16,16,128]{2,1,0:T(8,128)}), f32[16,16,128]{2,1,0:T(8,128)S(1)}, u32[]{:S(2)}, u32[]{:S(2)}) async-start(f32[16,16,128]{2,1,0:T(8,128)} %mix_coarse_kernel.1), calls=%async_computation.3 | async-start | bytes 262144 | tf_op jit(solution)/shard_map/all_to_all | solution.py:512
  77.0 0.0 copy-start.2
  77.0 2.3 %copy-done.2 = f32[48,2,96,128]{3,2,1,0:T(8,128)S(1)} copy-done((f32[48,2,96,128]{3,2,1,0:T(8,128)S(1)}, f32[48,2,96,128]{3,2,1,0:T(8,128)}, u32[]{:S(2)}) %copy-start.2) | copy-done | bytes 4718616
  79.3 2.3 %copy-done.9 = f32[48,2,96,128]{3,2,1,0:T(8,128)S(1)} copy-done((f32[48,2,96,128]{3,2,1,0:T(8,128)S(1)}, f32[48,2,96,128]{3,2,1,0:T(8,128)}, u32[]{:S(2)}) %copy-start.9) | copy-done | bytes 4718616
  81.7 0.0 copy-start.15
  81.7 4.3 %project_kernel.1.base_ref = f32[48,2,96,128]{3,2,1,0:T(8,128)S(1)} custom-call(f32[48,2,96,128]{3,2,1,0:T(8,128)S(1)} %copy-done.9, f32[48,48]{1,0:T(8,128)S(1)} %copy-done.17, f32[48,2,96,128]{3,2,1,0:T(8,128)S(1)} %copy-done.2), custom_call_target="tpu_custom_call" | custom-call | tf_op jit(solution)/shard_map/project_kernel/pallas_call | solution.py:55
  86.0 0.0 copy-start.5
  86.0 2.2 %copy-done.5 = f32[48,2,96,128]{3,2,1,0:T(8,128)} copy-done((f32[48,2,96,128]{3,2,1,0:T(8,128)}, f32[48,2,96,128]{3,2,1,0:T(8,128)S(1)}, u32[]{:S(2)}) %copy-start.5) | copy-done | bytes 4718616
  88.2 0.0 copy-done.19
  88.2 2.5 %lift_coarse_kernel.1.lift_ref = f32[144,1024]{1,0:T(8,128)S(1)} custom-call(f32[48,48,128]{2,1,0:T(8,128)S(1)} %get-tuple-element.9.v_ref, f32[48,48]{1,0:T(8,128)S(1)} %copy-done.23, bf16[256,128]{1,0:T(8,128)(2,1)S(1)} %copy-done.19), custom_call_target="tpu_custom_call" | custom-call | tf_op jit(solution)/shard_map/lift_coarse_kernel/pallas_call | solution.py:55
  90.6 0.0 all-to-all-done.3
  90.6 0.0 copy-done.11
  90.7 0.0 copy-done.14
  90.7 0.0 copy-done.15
  90.7 0.0 copy-start.6
  90.7 2.3 %copy-done.6 = f32[48,2,96,128]{3,2,1,0:T(8,128)S(1)} copy-done((f32[48,2,96,128]{3,2,1,0:T(8,128)S(1)}, f32[48,2,96,128]{3,2,1,0:T(8,128)}, u32[]{:S(2)}) %copy-start.6) | copy-done | bytes 4718616
  93.0 5.3 %finish.1 = f32[48,2,96,128]{3,2,1,0:T(8,128)} custom-call(f32[256,128]{1,0:T(8,128)S(1)} %bitcast.8, f32[144,1024]{1,0:T(8,128)S(1)} %lift_coarse_kernel.1.lift_ref, f32[48,2,96,128]{3,2,1,0:T(8,128)S(1)} %copy-done.6, f32[48,48]{1,0:T(8,128)S(1)} %copy-done.17, bf16[2,288,256]{2,1,0:T(8,128)(2,1)S(1)} %copy-done.11, bf16[2,256,128]{2,1,0:T(8,128)(2,1)S(1)} %copy-done.15, ...), custom_call_target="tpu_custom_call" | custom-call | tf_op jit(solution)/shard_map/finish/pallas_call | solution.py:55
  (16 shorter events, 0.0 us)
Async XLA Ops:
  0.0 2.3 %copy-start = (f32[48,2,96,128]{3,2,1,0:T(8,128)S(1)}, f32[48,2,96,128]{3,2,1,0:T(8,128)}, u32[]{:S(2)}) copy-start(f32[48,2,96,128]{3,2,1,0:T(8,128)} %base_ref.1) | copy-start | bytes 14155780
  2.3 0.9 copy-start.13
  3.3 0.8 copy-start.22
  4.1 26.0 %copy-start.7 = (bf16[96,8,48,48]{0,3,2,1:T(8,128)(2,1)S(1)}, bf16[96,8,48,48]{0,3,2,1:T(8,128)(2,1)}, u32[]{:S(2)}) copy-start(bf16[96,8,48,48]{0,3,2,1:T(8,128)(2,1)} %param.18) | copy-start | bytes 10616836
  4.1 26.0 %copy-start.18 = (f32[128,128]{1,0:T(8,128)S(1)}, f32[128,128]{1,0:T(8,128)}, u32[]{:S(2)}) copy-start(f32[128,128]{1,0:T(8,128)} %constant.24.clone.tv_ref) | copy-start | bytes 196612
  5.7 31.0 %copy-start.24 = (f32[48,48]{1,0:T(8,128)S(1)}, f32[48,48]{1,0:T(8,128)}, u32[]{:S(2)}) copy-start(f32[48,48]{1,0:T(8,128)} %a_ref.4) | copy-start | bytes 27652
  33.0 19.1 %all-to-all-start.1 = ((f32[16,72,128]{2,1,0:T(8,128)}), f32[16,72,128]{2,1,0:T(8,128)S(1)}, u32[]{:S(2)}, u32[]{:S(2)}) async-start(f32[16,72,128]{2,1,0:T(8,128)} %mix_fine.1), calls=%async_computation.1 | async-start | bytes 1179648 | tf_op jit(solution)/shard_map/all_to_all | solution.py:512
  36.6 2.3 %copy-start.1 = (f32[48,2,96,128]{3,2,1,0:T(8,128)S(1)}, f32[48,2,96,128]{3,2,1,0:T(8,128)}, u32[]{:S(2)}) copy-start(f32[48,2,96,128]{3,2,1,0:T(8,128)} %base_ref.1) | copy-start | bytes 14155780
  39.0 13.1 %copy-start.12 = (bf16[256,512]{1,0:T(8,128)(2,1)S(1)}, bf16[256,512]{1,0:T(8,128)(2,1)}, u32[]{:S(2)}) copy-start(bf16[256,512]{1,0:T(8,128)(2,1)} %constant.26.clone.refs_3_) | copy-start | bytes 786436
  39.0 13.1 %copy-start.16 = (bf16[2,128,256]{2,1,0:T(8,128)(2,1)S(1)}, bf16[2,128,256]{2,1,0:T(8,128)(2,1)}, u32[]{:S(2)}) copy-start(bf16[2,128,256]{2,1,0:T(8,128)(2,1)} %constant.28.clone.refs_5_) | copy-start | bytes 393220
  39.0 13.1 %copy-start.20 = (bf16[96,192]{1,0:T(8,128)(2,1)S(1)}, bf16[96,192]{1,0:T(8,128)(2,1)}, u32[]{:S(2)}) copy-start(bf16[96,192]{1,0:T(8,128)(2,1)} %constant.27.clone.refs_4_) | copy-start | bytes 110596
  39.0 13.1 %copy-start.21 = (bf16[96,144]{1,0:T(8,128)(2,1)S(1)}, bf16[96,144]{1,0:T(8,128)(2,1)}, u32[]{:S(2)}) copy-start(bf16[96,144]{1,0:T(8,128)(2,1)} %constant.25.clone.refs_2_) | copy-start | bytes 82948
  39.0 33.0 %copy-start.10 = (bf16[24,4,48,48]{3,2,1,0:T(8,128)(2,1)S(1)}, bf16[24,4,48,48]{3,2,1,0:T(8,128)(2,1)}, u32[]{:S(2)}) copy-start(bf16[24,4,48,48]{3,2,1,0:T(8,128)(2,1)} %refs_1_.1) | copy-start | bytes 1327108
  39.0 38.0 %copy-start.17 = (f32[48,48]{1,0:T(8,128)S(1)}, f32[48,48]{1,0:T(8,128)}, u32[]{:S(2)}) copy-start(f32[48,48]{1,0:T(8,128)} %a_ref.7) | copy-start | bytes 27652
  43.3 2.2 %copy-start.3 = (f32[48,2,96,128]{3,2,1,0:T(8,128)}, f32[48,2,96,128]{3,2,1,0:T(8,128)S(1)}, u32[]{:S(2)}) copy-start(f32[48,2,96,128]{3,2,1,0:T(8,128)S(1)} %lift_fine_kernel.1.refs_1_) | copy-start | bytes 14155780
  52.1 2.3 %copy-start.4 = (f32[48,2,96,128]{3,2,1,0:T(8,128)S(1)}, f32[48,2,96,128]{3,2,1,0:T(8,128)}, u32[]{:S(2)}) copy-start(f32[48,2,96,128]{3,2,1,0:T(8,128)} %copy-done.3) | copy-start | bytes 14155780
  57.8 2.2 %copy-start.8 = (f32[48,2,96,128]{3,2,1,0:T(8,128)}, f32[48,2,96,128]{3,2,1,0:T(8,128)S(1)}, u32[]{:S(2)}) copy-start(f32[48,2,96,128]{3,2,1,0:T(8,128)S(1)} %get-tuple-element.10.v_ref) | copy-start | bytes 14155780
  73.3 17.4 %all-to-all-start.3 = ((f32[16,16,128]{2,1,0:T(8,128)}), f32[16,16,128]{2,1,0:T(8,128)S(1)}, u32[]{:S(2)}, u32[]{:S(2)}) async-start(f32[16,16,128]{2,1,0:T(8,128)} %mix_coarse_kernel.1), calls=%async_computation.3 | async-start | bytes 262144 | tf_op jit(solution)/shard_map/all_to_all | solution.py:512
  77.0 2.3 %copy-start.2 = (f32[48,2,96,128]{3,2,1,0:T(8,128)S(1)}, f32[48,2,96,128]{3,2,1,0:T(8,128)}, u32[]{:S(2)}) copy-start(f32[48,2,96,128]{3,2,1,0:T(8,128)} %base_ref.1) | copy-start | bytes 14155780
  79.3 2.3 %copy-start.9 = (f32[48,2,96,128]{3,2,1,0:T(8,128)S(1)}, f32[48,2,96,128]{3,2,1,0:T(8,128)}, u32[]{:S(2)}) copy-start(f32[48,2,96,128]{3,2,1,0:T(8,128)} %copy-done.8) | copy-start | bytes 14155780
  81.7 6.5 %copy-start.19 = (bf16[256,128]{1,0:T(8,128)(2,1)S(1)}, bf16[256,128]{1,0:T(8,128)(2,1)}, u32[]{:S(2)}) copy-start(bf16[256,128]{1,0:T(8,128)(2,1)} %constant.29.clone.pz_ref) | copy-start | bytes 196612
  81.7 6.5 %copy-start.23 = (f32[48,48]{1,0:T(8,128)S(1)}, f32[48,48]{1,0:T(8,128)}, u32[]{:S(2)}) copy-start(f32[48,48]{1,0:T(8,128)} %a_ref.5) | copy-start | bytes 27652
  81.7 9.0 %copy-start.11 = (bf16[2,288,256]{2,1,0:T(8,128)(2,1)S(1)}, bf16[2,288,256]{2,1,0:T(8,128)(2,1)}, u32[]{:S(2)}) copy-start(bf16[2,288,256]{2,1,0:T(8,128)(2,1)} %constant.30.clone.yi_ref) | copy-start | bytes 884740
  81.7 9.0 %copy-start.14 = (bf16[256,256]{1,0:T(8,128)(2,1)S(1)}, bf16[256,256]{1,0:T(8,128)(2,1)}, u32[]{:S(2)}) copy-start(bf16[256,256]{1,0:T(8,128)(2,1)} %constant.32.clone.up_ref) | copy-start | bytes 393220
  81.7 9.0 %copy-start.15 = (bf16[2,256,128]{2,1,0:T(8,128)(2,1)S(1)}, bf16[2,256,128]{2,1,0:T(8,128)(2,1)}, u32[]{:S(2)}) copy-start(bf16[2,256,128]{2,1,0:T(8,128)(2,1)} %constant.31.clone.ei_ref) | copy-start | bytes 393220
  86.0 2.2 %copy-start.5 = (f32[48,2,96,128]{3,2,1,0:T(8,128)}, f32[48,2,96,128]{3,2,1,0:T(8,128)S(1)}, u32[]{:S(2)}) copy-start(f32[48,2,96,128]{3,2,1,0:T(8,128)S(1)} %project_kernel.1.base_ref) | copy-start | bytes 14155780
  90.7 2.3 %copy-start.6 = (f32[48,2,96,128]{3,2,1,0:T(8,128)S(1)}, f32[48,2,96,128]{3,2,1,0:T(8,128)}, u32[]{:S(2)}) copy-start(f32[48,2,96,128]{3,2,1,0:T(8,128)} %copy-done.5) | copy-start | bytes 14155780
where the time goes:
time: 99.1 us; the launch traced here: 98.5 us
  blocking collectives  36.4 us (37%)
  Pallas kernels  25.5 us (26%)
  local copies, waits for them, and re-layouts  22.4 us (23%)
  starting transfers between devices  7.27 us (7%)
  waiting for transfers between devices  6.63 us (7%)
    all_to_all x2, blocking collectives, swap(): return lax.all_to_all(blocks, 'gx', split_axis=0, concat_axis=0, tiled=True)  36.4 us
    pallas_call x8, Pallas kernels, vmem_call(): pl.pallas_call(body, out_shape=shapes[0] if single else shapes, in_specs=...  25.5 us
    unnamed x50, local copies, waits for them, and re-layouts  22.4 us
    all_to_all x2, starting transfers between devices, swap(): return lax.all_to_all(blocks, 'gx', split_axis=0, concat_axis=0, tiled=True)  7.27 us
    all_to_all x2, waiting for transfers between devices, swap(): return lax.all_to_all(blocks, 'gx', split_axis=0, concat_axis=0, tiled=True)  6.63 us
  transfers between devices with their start and end apart: 2, of which 1 were waited for; matrix products, arithmetic and copies ran while one was open for 0% of the time, Pallas kernels for 11%

commit v1 on v0

v1 whole, which is shorter than its diff:
```python
import jax
import jax.numpy as jnp
import numpy as np
from jax import lax
from jax.experimental import pallas as pl
from jax.experimental.pallas import tpu as pltpu
from jax.sharding import PartitionSpec as P

KY = 48
KZ = 32
LANES = 128
PAD = 16
GROUP = 16
HIGHEST = lax.Precision.HIGHEST
BF = jnp.bfloat16
F32 = jnp.float32
MIB = 1 << 20
LIFT_FLOPS = 1 << 32
FETCHES = 3


def cosine(modes_kept, length):
    orders = np.arange(modes_kept)[:, None]
    points = np.arange(length)[None, :]
    phase = orders * (2 * points + 1) % (4 * length)
    scales = np.where(orders == 0, np.sqrt(1.0 / length), np.sqrt(2.0 / length))
    return scales * np.cos(np.pi / (2 * length) * phase)


def halves(table):
    table = np.asarray(table, np.float32)
    high = table.astype(BF)
    low = (table - high.astype(np.float32)).astype(BF)
    return high, low


def split(values):
    high = values.astype(BF)
    return high, (values - high.astype(F32)).astype(BF)


def dot(a, b):
    return jnp.dot(a, b, preferred_element_type=F32)


def gelu(t):
    return 0.5 * t * (1.0 + lax.erf(t * np.float32(np.sqrt(0.5))))


def paired(values):
    return values.reshape((2, values.shape[0] // 2) + values.shape[1:])


def vmem_call(body, outs, args, scratch, limit, flops=0, in_hbm=(), out_hbm=()):
    specs = [
        pl.BlockSpec(memory_space=pltpu.HBM if n in in_hbm else pltpu.VMEM) for n in range(len(args))
    ]
    out_specs = [
        pl.BlockSpec(memory_space=pltpu.HBM if n in out_hbm else pltpu.VMEM) for n in range(len(outs))
    ]
    shapes = [
        pltpu.HBM(shape, kind) if n in out_hbm else jax.ShapeDtypeStruct(shape, kind)
        for n, (shape, kind) in enumerate(outs)
    ]
    args = [
        pltpu.with_memory_space_constraint(a, pltpu.HBM) if n in in_hbm else a
        for n, a in enumerate(args)
    ]
    moved = sum(a.size * a.dtype.itemsize for a in args)
    result = pl.pallas_call(
        body,
        out_shape=shapes,
        in_specs=specs,
        out_specs=out_specs,
        scratch_shapes=scratch,
        compiler_params=pltpu.CompilerParams(vmem_limit_bytes=limit * MIB),
        cost_estimate=pl.CostEstimate(flops=flops, transcendentals=0, bytes_accessed=moved),
    )(*args)
    return result[0] if len(outs) == 1 else result


def interleave_matrix(matrix):
    channels = matrix.shape[0]
    size = channels * 8
    spread = (
        lax.broadcasted_iota(jnp.int32, (channels, size), 1) // 8
        == lax.broadcasted_iota(jnp.int32, (channels, size), 0)
    ).astype(F32).astype(BF)
    keep = (
        lax.broadcasted_iota(jnp.int32, (size, size), 0) % 8
        == lax.broadcasted_iota(jnp.int32, (size, size), 1) % 8
    )
    first = (((0,), (0,)), ((), ()))
    parts = []
    for part in split(matrix):
        tall = lax.dot_general(part, spread, first, preferred_element_type=F32).astype(BF)
        wide = lax.dot_general(spread, tall, first, preferred_element_type=F32)
        parts.append(jnp.where(keep, wide, 0.0).astype(BF))
    return parts


def forward_fine(hbm_ref, wz_hbm, ty_hbm, out_ref, z_ref, v_ref, wz_ref, ty_ref, sems):
    _, half, local_x, cells_y, _ = v_ref.shape
    steps = FETCHES
    chunk = half // steps
    tables = [
        pltpu.make_async_copy(wz_hbm, wz_ref, sems.at[steps]),
        pltpu.make_async_copy(ty_hbm, ty_ref, sems.at[steps + 1]),
    ]
    fetches = [
        pltpu.make_async_copy(hbm_ref.at[:, span], v_ref.at[:, span], sems.at[n])
        for n, span in enumerate(pl.ds(n * chunk, chunk) for n in range(steps))
    ]
    for copy in [tables[0], fetches[0], tables[1]] + fetches[1:]:
        copy.start()
    modes_y = ty_ref.shape[0] // 2

    def along_z(first):
        rows = [
            jnp.concatenate([v_ref[c2, cp, x] for c2 in range(2) for x in range(local_x)], axis=1)
            for cp in range(first, first + chunk)
        ]
        high, low = split(jnp.concatenate(rows, axis=0))
        wide = dot(high, wz_ref[...])
        total = wide[:, :LANES] + wide[:, LANES:] + dot(low, wz_ref[:, :LANES])
        for m in range(chunk):
            z_ref[first + m] = total[m * cells_y : (m + 1) * cells_y]

    def along_y(first):
        for cp in range(first, first + chunk, 2):
            high, low = split(jnp.concatenate([z_ref[cp], z_ref[cp + 1]], axis=1))
            both = dot(ty_ref[...], jnp.concatenate([high, low], axis=0))
            both = both[:modes_y] + both[modes_y:]
            for n in range(2):
                out_ref[pl.ds(cp + n, modes_y, stride=half), :] = both[
                    :, n * LANES : (n + 1) * LANES
                ]

    tables[0].wait()
    for n in range(steps):
        fetches[n].wait()
        if n == 1:
            tables[1].wait()
        if n:
            along_y((n - 1) * chunk)
        along_z(n * chunk)
    along_y((steps - 1) * chunk)


def fine_coefficients(features):
    channels, local_x, cells_y, cells_z = features.shape
    high, low = halves(cosine(KZ, cells_z).T)
    eye = np.eye(2 * local_x, dtype=np.float32)
    wz = np.concatenate(
        [np.kron(eye, part.astype(np.float32)) for part in (high, low)], axis=1
    ).astype(BF)
    high, low = halves(cosine(KY, cells_y))
    ty = np.block([[high, high], [low, np.zeros_like(low)]]).astype(BF)
    return vmem_call(
        forward_fine,
        [((KY * channels // 2, LANES), F32)],
        (paired(features), jnp.asarray(wz), jnp.asarray(ty)),
        [
            pltpu.VMEM((channels // 2, cells_y, LANES), F32),
            pltpu.VMEM(paired(features).shape, F32),
            pltpu.VMEM(wz.shape, BF),
            pltpu.VMEM(ty.shape, BF),
            pltpu.SemaphoreType.DMA((FETCHES + 2,)),
        ],
        16,
        in_hbm=(0, 1, 2),
    )


def mix_fine(r_ref, w_ref, tv_ref, out_ref, modal_ref, mixed_ref, spread_ref):
    members, _, _ = r_ref.shape
    modes_x, channels, _, owned = w_ref.shape
    half = channels // 2
    per = owned // KZ
    quarter = lax.broadcasted_iota(jnp.int32, (half, LANES), 1) // KZ
    for first in range(0, modes_x, 4):
        acc = [None] * 4
        for a in range(members):
            block = r_ref[a]
            for n in range(4):
                term = block * tv_ref[(first + n) * members + a][None, :]
                acc[n] = term if a == 0 else acc[n] + term
        for n in range(4):
            both = acc[n] + pltpu.roll(acc[n], LANES - KZ, 1)
            for c2 in range(2):
                placed = None
                for i in range(per):
                    piece = both[i * half : (i + 1) * half]
                    shift = (KZ * i - 2 * KZ * c2) % LANES
                    piece = pltpu.roll(piece, shift, 1) if shift else piece
                    placed = piece if placed is None else jnp.where(quarter == i, piece, placed)
                modal_ref[first + n, c2 * half : (c2 + 1) * half, :] = placed.astype(BF).astype(F32)

    def one_mode(k, carry):
        total = None
        for c in range(channels):
            term = modal_ref[k, c : c + 1, :owned] * w_ref[k, c].astype(F32)
            total = term if total is None else total + term
        mixed_ref[k, :, :owned] = total
        return carry

    lax.fori_loop(0, modes_x, one_mode, 0)
    for k in range(modes_x):
        for i in range(per):
            placed = None
            for q in range(4):
                c2 = q // 2
                piece = mixed_ref[k, c2 * half : (c2 + 1) * half, :]
                shift = (KZ * q - KZ * i) % LANES
                piece = pltpu.roll(piece, shift, 1) if shift else piece
                placed = piece if placed is None else jnp.where(quarter == q, piece, placed)
            spread_ref[k, i * half : (i + 1) * half, :] = placed
    for a in range(members):
        total = None
        for k in range(modes_x):
            term = spread_ref[k] * tv_ref[k * members + a][None, :]
            total = term if total is None else total + term
        out_ref[a] = total


def fine_mixed(received, weights, local_x):
    members, rows, _ = received.shape
    _, modes_x, channels, _ = weights.shape
    table = cosine(modes_x, members * local_x).reshape(modes_x * members, local_x)
    lanes = np.tile(np.repeat(table, KZ, axis=1), (1, 2)).astype(np.float32)
    return vmem_call(
        mix_fine,
        [(received.shape, F32)],
        (received, jnp.transpose(weights, (1, 2, 3, 0)), jnp.asarray(lanes)),
        [
            pltpu.VMEM((modes_x, channels, LANES), F32),
            pltpu.VMEM((modes_x, channels, LANES), F32),
            pltpu.VMEM((modes_x, rows, LANES), F32),
        ],
        16,
    )


def lift_block(source, parts, y, store):
    channels = source.shape[0]
    block = jnp.concatenate(
        [source[:, y + s : y + s + 8, :].reshape(channels * 8, LANES) for s in (0, 8)], axis=1
    )
    high, low = split(block)
    done = dot(parts[0], high) + dot(parts[1], high) + dot(parts[0], low)
    for n in range(2):
        store(y + 8 * n, done[:, n * LANES : (n + 1) * LANES].reshape(channels, 8, LANES))


def stripes(source, target, sems, first, step):
    copies = []
    for n, y in enumerate(range(0, source.shape[-2], step)):
        span = (slice(None),) * (len(source.shape) - 2) + (pl.ds(y, step), slice(None))
        copies.append(pltpu.make_async_copy(source.at[span], target.at[span], sems.at[first + n]))
    return copies


def coarse_table(table_ref, out_ref):
    lane = lax.broadcasted_iota(jnp.int32, table_ref.shape[1:], 1) % GROUP
    cells_z = table_ref.shape[1]
    for c in range(GROUP):
        for part in range(2):
            out_ref[part, c * cells_z : (c + 1) * cells_z, :] = jnp.where(
                lane == c, table_ref[part].astype(F32), 0.0
            ).astype(BF)


def lift_fine_kernel(hbm_ref, a_ref, ec_ref, out_hbm, w_ref, v_ref, out_ref, sems):
    _, local_x, _, _ = v_ref.shape
    fetches = stripes(hbm_ref, v_ref, sems, 0, 32)
    stores = stripes(out_ref, out_hbm, sems, len(fetches), 32)
    for copy in fetches:
        copy.start()
    coarse_table(ec_ref, w_ref)
    parts = interleave_matrix(a_ref[...])
    for n in range(len(fetches)):
        fetches[n].wait()
        for x in range(local_x):
            def store(at, value, x=x):
                out_ref[:, x, at : at + 8, :] = value

            for y in range(32 * n, 32 * n + 32, 16):
                lift_block(v_ref.at[:, x], parts, y, store)
        stores[n].start()
    for copy in stores:
        copy.wait()


def project_kernel(hbm_ref, a_ref, base_hbm, out_hbm, v_ref, base_ref, sems):
    _, local_x, cells_y, _ = v_ref.shape
    steps = cells_y // 32
    fetches = stripes(hbm_ref, v_ref, sems, 0, 32)
    bases = stripes(base_hbm, base_ref, sems, steps, 32)
    stores = stripes(base_ref, out_hbm, sems, 2 * steps, 32)
    for n in range(steps):
        fetches[n].start()
        bases[n].start()
    parts = interleave_matrix(a_ref[...])
    for n in range(steps):
        fetches[n].wait()
        bases[n].wait()
        for x in range(local_x):
            def store(at, value, x=x):
                base_ref[:, x, at : at + 8, :] += value

            for y in range(32 * n, 32 * n + 32, 16):
                lift_block(v_ref.at[:, x], parts, y, store)
        stores[n].start()
    for copy in stores:
        copy.wait()


def fine_lifted(features, matrix):
    _, _, cells_y, cells_z = features.shape
    coarse_z = cells_z // 2
    pool_z = np.kron(np.eye(coarse_z), np.ones((1, 2))) / 2.0
    ec = np.repeat((cosine(KZ // 2, coarse_z) @ pool_z).T, GROUP, axis=1)
    ec = np.stack(halves(ec))
    return vmem_call(
        lift_fine_kernel,
        [(features.shape, F32), ((2, GROUP * cells_z, 2 * LANES), BF)],
        (features, matrix, jnp.asarray(ec)),
        [
            pltpu.VMEM(features.shape, F32),
            pltpu.VMEM(features.shape, F32),
            pltpu.SemaphoreType.DMA((cells_y // 16,)),
        ],
        20,
        LIFT_FLOPS,
        in_hbm=(0,),
        out_hbm=(0,),
    )


def projected(level_one, matrix, features):
    cells_y = features.shape[2]
    return vmem_call(
        project_kernel,
        [(features.shape, F32)],
        (level_one, matrix, features),
        [
            pltpu.VMEM(features.shape, F32),
            pltpu.VMEM(features.shape, F32),
            pltpu.SemaphoreType.DMA((3 * cells_y // 32,)),
        ],
        20,
        LIFT_FLOPS,
        in_hbm=(0, 2),
        out_hbm=(0,),
    )


def lift_coarse_kernel(hbm_ref, a_ref, pz_ref, o_ref, ei_ref, out_ref, parts_ref, b_ref, p_ref, v_ref, sem):
    fetch = pltpu.make_async_copy(hbm_ref, v_ref, sem)
    fetch.start()
    parts = interleave_matrix(o_ref[...])
    parts_ref[0] = parts[0]
    parts_ref[1] = parts[1]
    parts = interleave_matrix(a_ref[...])
    fetch.wait()
    channels, cells_y, _ = v_ref.shape

    def store(y, value):
        p_ref[:, y : y + 8, :] = value

    for y in range(0, cells_y, 16):
        lift_block(v_ref, parts, y, store)
    rows = jnp.concatenate(
        [jnp.concatenate([p_ref[c], p_ref[c + 1]], axis=1) for c in range(0, channels, 2)], axis=0
    )
    high, low = split(rows)
    done = dot(high, pz_ref[...]) + dot(low, pz_ref[...])
    for cg in range(channels // GROUP):
        for t in range(GROUP // 2):
            n = cg * (GROUP // 2) + t
            out_ref[cg * cells_y : (cg + 1) * cells_y, t * LANES : (t + 1) * LANES] = done[
                n * cells_y : (n + 1) * cells_y
            ]
    coarse_z = pz_ref.shape[1] // 2
    lane = lax.broadcasted_iota(jnp.int32, (2 * LANES, LANES), 1) // coarse_z
    row = lax.broadcasted_iota(jnp.int32, (2 * LANES, LANES), 0) % GROUP
    for t in range(GROUP // 2):
        for part in range(2):
            b_ref[part, :, t * LANES : (t + 1) * LANES] = jnp.where(
                row == 2 * t + lane, ei_ref[part].astype(F32), 0.0
            ).astype(BF)


def coarse_lifted(pool_y, lift_middle, project_out):
    channels, coarse_y, cells_z = pool_y.shape
    coarse_z = cells_z // 2
    pool_z = np.kron(np.eye(coarse_z), np.ones((1, 2))).T / 2.0
    pool_z = np.kron(np.eye(2), pool_z).astype(BF)
    inverse_z = np.repeat(cosine(KZ // 2, coarse_z), GROUP, axis=0)
    ei = np.stack(halves(np.concatenate([inverse_z] * (LANES // coarse_z), axis=1)))
    wide = GROUP // 2 * LANES
    return vmem_call(
        lift_coarse_kernel,
        [
            ((channels // GROUP * coarse_y, wide), F32),
            ((2, channels * 8, channels * 8), BF),
            ((2, 2 * LANES, wide), BF),
        ],
        (pool_y, lift_middle, jnp.asarray(pool_z), project_out, jnp.asarray(ei)),
        [
            pltpu.VMEM(pool_y.shape, F32),
            pltpu.VMEM(pool_y.shape, F32),
            pltpu.SemaphoreType.DMA,
        ],
        12,
        LIFT_FLOPS // 2,
        in_hbm=(0,),
    )


def inverse_fine(r_ref, lift_hbm, ty_ref, bz_ref, yc_ref, w_ref, level_hbm, pool_hbm, out_ref,
                 g_ref, q_ref, d_ref, lift_ref, level_ref, tall_ref, pool_ref, sems, place):
    _, half, local_x, cells_y, _ = lift_ref.shape
    modes_y = r_ref.shape[0] // half
    half_ky = modes_y // 2
    steps = FETCHES
    chunk = half // steps
    spans = [pl.ds(n * chunk, chunk) for n in range(steps)]
    fetches = [
        pltpu.make_async_copy(lift_hbm.at[:, span], lift_ref.at[:, span], sems.at[n])
        for n, span in enumerate(spans)
    ]
    stores = [
        pltpu.make_async_copy(level_ref.at[:, span], level_hbm.at[:, span], sems.at[steps + n])
        for n, span in enumerate(spans)
    ]
    pool = pltpu.make_async_copy(pool_ref, pool_hbm, sems.at[2 * steps])
    for copy in fetches:
        copy.start()
    for cp in range(0, half, 2):
        block = jnp.concatenate(
            [r_ref[pl.ds(cp + n, modes_y, stride=half), :] for n in range(2)], axis=1
        )
        high, low = split(block)
        both = dot(ty_ref[...], jnp.concatenate([high, low, high], axis=0)).astype(BF)
        for n in range(2):
            part = both[:, n * LANES : (n + 1) * LANES]
            g_ref[(cp + n) * cells_y : (cp + n + 1) * cells_y, :] = jnp.concatenate(
                [part, part], axis=1
            )
    for step in range(steps):
        first = step * chunk
        fetches[step].wait()
        wide = dot(g_ref[first * cells_y : (first + chunk) * cells_y, :], bz_ref[...])
        for n in range(chunk):
            cp = first + n
            for c2 in range(2):
                for x in range(local_x):
                    q = c2 * local_x + x
                    piece = wide[n * cells_y : (n + 1) * cells_y, q * LANES : (q + 1) * LANES]
                    piece = gelu(piece + lift_ref[c2, cp, x])
                    level_ref[c2, cp, x] = piece
                    tall_ref[cp, x * cells_y : (x + 1) * cells_y, c2 * LANES : (c2 + 1) * LANES] = (
                        piece.astype(BF)
                    )
        stores[step].start()
    for cp in range(half):
        down = dot(yc_ref[...], tall_ref[cp])
        for c2 in range(2):
            c = cp + c2 * half
            cg, inner = c // GROUP, c % GROUP
            part = down[:, c2 * LANES : (c2 + 1) * LANES]
            q_ref[cg * half_ky : (cg + 1) * half_ky, inner * LANES : (inner + 1) * LANES] = (
                part[:half_ky] + part[half_ky : 2 * half_ky]
            )
            pool_ref[c] = part[2 * half_ky :]
    pool.start()
    high, low = split(q_ref[...])
    d_ref[...] = dot(high, w_ref[0]) + dot(low, w_ref[0]) + dot(high, w_ref[1])
    out_ref[...] = jnp.zeros_like(out_ref)
    for (cg, jh, i), row in place.items():
        source = cg * half_ky + i
        out_ref[row : row + 1, :] = d_ref[source : source + 1, jh * LANES : (jh + 1) * LANES]
    for copy in stores:
        copy.wait()
    pool.wait()


def fine_level(received, lifted, table_z, place, place_rows):
    channels, local_x, cells_y, cells_z = lifted.shape
    half_ky = KY // 2
    coarse_y = cells_y // 2
    high, low = halves(cosine(KY, cells_y).T)
    ty = np.concatenate([high, high, low], axis=1)
    eye = np.eye(2 * local_x, dtype=np.float32)
    bz = np.concatenate(
        [np.kron(eye, part.astype(np.float32)) for part in halves(cosine(KZ, cells_z))], axis=0
    ).astype(BF)
    pool_y = np.kron(np.eye(coarse_y), np.ones((1, 2))) / (2.0 * local_x)
    high, low = halves(cosine(half_ky, coarse_y) @ pool_y)
    yc = np.concatenate([high, low, pool_y.astype(BF)], axis=0)
    yc = np.concatenate([yc] * local_x, axis=1)
    groups = channels // GROUP

    def inverse_fine_kernel(*refs):
        inverse_fine(*refs, place)

    whole = paired(lifted).shape
    level, pooled, coarse = vmem_call(
        inverse_fine_kernel,
        [(whole, F32), ((channels, coarse_y, cells_z), F32), ((place_rows, LANES), F32)],
        (received, paired(lifted), jnp.asarray(ty), jnp.asarray(bz), jnp.asarray(yc), table_z),
        [
            pltpu.VMEM((channels // 2 * cells_y, 2 * LANES), BF),
            pltpu.VMEM((groups * half_ky, GROUP * cells_z), F32),
            pltpu.VMEM((groups * half_ky, 2 * LANES), F32),
            pltpu.VMEM(whole, F32),
            pltpu.VMEM(whole, F32),
            pltpu.VMEM((channels // 2, local_x * cells_y, 2 * LANES), BF),
            pltpu.VMEM((channels, coarse_y, cells_z), F32),
            pltpu.SemaphoreType.DMA((2 * FETCHES + 1,)),
        ],
        24,
        in_hbm=(1,),
        out_hbm=(0, 1),
    )
    return level.reshape(lifted.shape), pooled, coarse


def mix_coarse(r_ref, w_ref, out_ref, table, rows):
    members, pad, _ = r_ref.shape
    owned, modes_x, channels, _ = w_ref.shape
    groups = channels // GROUP
    inner = LANES // GROUP
    units = owned // inner
    lane = lax.broadcasted_iota(jnp.int32, (rows, LANES), 1)
    row = lax.broadcasted_iota(jnp.int32, (rows, channels), 0)
    modal = []
    for k in range(modes_x):
        total = None
        for a in range(members):
            term = r_ref[a] * float(table[k, a])
            total = term if total is None else total + term
        modal.append(total)
    fill = jnp.zeros((rows - modes_x * units, LANES), F32)
    packed = [
        jnp.concatenate(
            [modal[k][cg * units : (cg + 1) * units] for k in range(modes_x)] + [fill], axis=0
        )
        for cg in range(groups)
    ]
    mixed = []
    for j in range(inner):
        placed = None
        for cg in range(groups):
            shift = (GROUP * cg - GROUP * j) % LANES
            piece = pltpu.roll(packed[cg], shift, 1) if shift else packed[cg]
            placed = piece if placed is None else jnp.where(lane // GROUP == cg, piece, placed)
        left = placed[:, :channels].astype(BF)
        total = jnp.zeros((rows, channels), F32)
        for k in range(modes_x):
            for u in range(units):
                full = dot(left, w_ref[u * inner + j, k])
                total = jnp.where(row == k * units + u, full, total)
        mixed.append(jnp.concatenate([total, jnp.zeros((rows, LANES - channels), F32)], axis=1))
    spread = []
    for cg in range(groups):
        placed = None
        for j in range(inner):
            shift = (GROUP * j - GROUP * cg) % LANES
            piece = pltpu.roll(mixed[j], shift, 1) if shift else mixed[j]
            placed = piece if placed is None else jnp.where(lane // GROUP == j, piece, placed)
        spread.append(placed)
    final = []
    for k in range(modes_x):
        final.append(
            jnp.concatenate(
                [spread[cg][k * units : (k + 1) * units] for cg in range(groups)]
                + [jnp.zeros((pad - groups * units, LANES), F32)],
                axis=0,
            )
        )
    for a in range(members):
        total = None
        for k in range(modes_x):
            term = final[k] * float(table[k, a])
            total = term if total is None else total + term
        out_ref[a] = total


def coarse_mixed(received, weights, coarse_x):
    owned, modes_x, _, _ = weights.shape
    table = cosine(modes_x, coarse_x)
    units = owned * GROUP // LANES
    rows = -(-modes_x * units // 16) * 16

    def mix_coarse_kernel(*refs):
        mix_coarse(*refs, table, rows)

    return vmem_call(mix_coarse_kernel, [(received.shape, F32)], (received, weights), [], 8)


def finish(r_ref, lift_ref, base_hbm, parts_ref, b_ref, yi_ref, up_ref, out_hbm, l_ref, u_ref, res_ref, sems):
    channels, local_x, cells_y, _ = res_ref.shape
    coarse_y = cells_y // 2
    groups = channels // GROUP
    fetches = stripes(base_hbm, res_ref, sems, 0, 32)
    stores = stripes(res_ref, out_hbm, sems, len(fetches), 32)
    for copy in fetches:
        copy.start()
    high, low = split(r_ref[...])
    grid = dot(yi_ref[0], high) + dot(yi_ref[0], low) + dot(yi_ref[1], high)
    left = jnp.concatenate(
        [
            jnp.concatenate(
                [grid[(2 * cg + jh) * coarse_y : (2 * cg + jh + 1) * coarse_y] for jh in range(2)],
                axis=1,
            )
            for cg in range(groups)
        ],
        axis=0,
    )
    high, low = split(left)
    level = dot(high, b_ref[0]) + dot(low, b_ref[0]) + dot(high, b_ref[1])
    level = gelu(level + lift_ref[...])
    for cg in range(groups):
        tall = jnp.concatenate(
            [
                level[cg * coarse_y : (cg + 1) * coarse_y, t * LANES : (t + 1) * LANES]
                for t in range(GROUP // 2)
            ],
            axis=0,
        )
        high, low = split(tall)
        wide = dot(jnp.concatenate([high, low], axis=1), up_ref[...])
        for t in range(GROUP // 2):
            for c2 in range(2):
                l_ref[cg * GROUP + 2 * t + c2] = wide[
                    t * coarse_y : (t + 1) * coarse_y, c2 * LANES : (c2 + 1) * LANES
                ]

    def store(y, value):
        for c in range(channels):
            for n in range(2):
                u_ref[pl.ds(c * cells_y + 2 * y + n, 8, stride=2), :] = value[c]

    parts = (parts_ref[0], parts_ref[1])
    lift_block(l_ref, parts, 0, store)
    for n, y in enumerate(range(0, coarse_y, 16)):
        fetches[n].wait()
        if y + 16 < coarse_y:
            lift_block(l_ref, parts, y + 16, store)
        for c in range(channels):
            piece = u_ref[c * cells_y + 2 * y : c * cells_y + 2 * y + 32, :]
            for x in range(local_x):
                res_ref[c, x, 2 * y : 2 * y + 32, :] += piece
        stores[n].start()
    for copy in stores:
        copy.wait()


def final_result(received, lifted, base, parts, inverse_z, place, place_rows):
    channels, _, cells_y, cells_z = base.shape
    half_ky = KY // 2
    coarse_y, coarse_z = cells_y // 2, cells_z // 2
    groups = channels // GROUP
    table_y = cosine(half_ky, coarse_y)
    left = np.zeros((groups, 2, coarse_y, place_rows))
    for (cg, jh, i), row in place.items():
        left[cg, jh, :, row] = table_y[i]
    yi = np.stack(halves(left.reshape(groups * 2 * coarse_y, place_rows)))
    up = np.kron(np.eye(2), np.kron(np.eye(coarse_z), np.ones((1, 2))))
    up = np.concatenate([up, up], axis=0).astype(BF)
    return vmem_call(
        finish,
        [(base.shape, F32)],
        (received, lifted, base, parts, inverse_z, jnp.asarray(yi), jnp.asarray(up)),
        [
            pltpu.VMEM((channels, coarse_y, cells_z), F32),
            pltpu.VMEM((channels * cells_y, LANES), F32),
            pltpu.VMEM(base.shape, F32),
            pltpu.SemaphoreType.DMA((2 * cells_y // 32,)),
        ],
        24,
        in_hbm=(2,),
        out_hbm=(0,),
    )


def swap(blocks):
    return lax.all_to_all(blocks, "gx", split_axis=0, concat_axis=0, tiled=True)


def plain_mix(coeffs, weights, cells_x):
    table_x = jnp.asarray(cosine(weights.shape[1], cells_x), F32)
    pencils = lax.all_to_all(coeffs, "gx", split_axis=0, concat_axis=1, tiled=True)
    modal = jnp.einsum("mxc,kx->mkc", pencils, table_x, precision=HIGHEST)
    mixed = jnp.einsum(
        "mkc,mkco->mko", modal.astype(BF), weights, preferred_element_type=F32
    )
    back = jnp.einsum("mkc,kx->mxc", mixed, table_x, precision=HIGHEST)
    return lax.all_to_all(back, "gx", split_axis=1, concat_axis=0, tiled=True)


def on_device(features, fine_weights, middle_weights, lift_fine, lift_middle, project_out):
    channels, local_x, _, _ = features.shape
    group_size = lax.axis_size("gx")
    cells_x = local_x * group_size
    half = channels // 2
    half_ky, half_kz = KY // 2, KZ // 2
    groups = channels // GROUP
    inner = LANES // GROUP

    coeffs = fine_coefficients(features)
    owned = fine_weights.shape[0]
    if owned % KZ == 0 and owned <= LANES:
        received = swap(coeffs.reshape(group_size, -1, LANES))
        mixed = fine_mixed(received, fine_weights, local_x)
        slabs = swap(mixed).reshape(coeffs.shape)
    else:
        modes = coeffs.reshape(KY, half, 2, local_x, KZ).transpose(0, 4, 3, 2, 1)
        slabs = plain_mix(modes.reshape(KY * KZ, local_x, channels), fine_weights, cells_x)
        slabs = slabs.reshape(KY, KZ, local_x, 2, half).transpose(0, 4, 3, 2, 1)
        slabs = slabs.reshape(coeffs.shape)
    lifted, table_z = fine_lifted(features, lift_fine)

    owned = middle_weights.shape[0]
    direct = owned % inner == 0 and groups * (owned // inner) <= PAD
    place = {}
    for cg in range(groups):
        for i in range(half_ky):
            for jh in range(2):
                if direct:
                    member, unit = divmod(2 * i + jh, owned // inner)
                    place[cg, jh, i] = member * PAD + cg * (owned // inner) + unit
                else:
                    place[cg, jh, i] = (jh * groups + cg) * half_ky + i
    place_rows = group_size * PAD if direct else 2 * groups * half_ky
    level_one, pool_y, coarse = fine_level(slabs, lifted, table_z, place, place_rows)
    base = projected(level_one, project_out, features)
    coarse_lift, parts, inverse_z = coarse_lifted(pool_y, lift_middle, project_out)
    coarse_x = cells_x // 2
    if direct:
        received = swap(coarse.reshape(group_size, PAD, LANES))
        mixed = coarse_mixed(received, middle_weights, coarse_x)
        slabs = swap(mixed).reshape(coarse.shape)
    else:
        modes = coarse.reshape(2, groups, half_ky, inner, GROUP).transpose(2, 0, 3, 1, 4)
        slabs = plain_mix(
            modes.reshape(half_ky * half_kz, 1, channels), middle_weights, coarse_x
        )
        slabs = slabs.reshape(half_ky, 2, inner, groups, GROUP).transpose(1, 3, 0, 2, 4)
        slabs = slabs.reshape(coarse.shape)
    return final_result(slabs, coarse_lift, base, parts, inverse_z, place, place_rows)


def solution(mesh):
    in_specs = (
        P(None, ("groups", "gx"), None, None),
        P("gx", None, None, None),
        P("gx", None, None, None),
        P(),
        P(),
        P(),
    )
    out_specs = P(None, ("groups", "gx"), None, None)

    return jax.shard_map(
        on_device, mesh=mesh, in_specs=in_specs, out_specs=out_specs, check_vma=False
    )
```

time: 99.1 us -> 91.6 us (0.924)
  local copies, waits for them, and re-layouts: 22.4 us -> 0.08 us
  Pallas kernels: 25.5 us -> 38.6 us
  waiting for transfers between devices: 6.63 us -> 8.32 us
    unnamed x50 -> x28, local copies, waits for them, and re-layouts: 22.4 us -> 0.08 us
    pallas_call x8, Pallas kernels: 25.5 us -> 38.6 us  [vmem_call(): pl.pallas_call(body, out_shape=shapes, in_specs=specs, out_specs=out_spec...]
    all_to_all x2, waiting for transfers between devices: 6.63 us -> 8.32 us  [swap(): return lax.all_to_all(blocks, 'gx', split_axis=0, concat_axis=0, tiled=True)]
  transfers between devices with their start and end apart: 2 -> 2, of which waited for: 1 -> 1; matrix products, arithmetic and copies ran while one was open for 0% -> 0% of each run, Pallas kernels for 11% -> 21%
where the time goes in v1:
time: 91.6 us; the launch traced here: 91.2 us
  Pallas kernels  38.6 us (42%)
  blocking collectives  36.5 us (40%)
  waiting for transfers between devices  8.32 us (9%)
  starting transfers between devices  7.28 us (8%)
    pallas_call x8, Pallas kernels, vmem_call(): pl.pallas_call(body, out_shape=shapes, in_specs=specs, out_specs=out_spec...  38.6 us
    all_to_all x2, blocking collectives, swap(): return lax.all_to_all(blocks, 'gx', split_axis=0, concat_axis=0, tiled=True)  36.5 us
    all_to_all x2, waiting for transfers between devices, swap(): return lax.all_to_all(blocks, 'gx', split_axis=0, concat_axis=0, tiled=True)  8.32 us
    all_to_all x2, starting transfers between devices, swap(): return lax.all_to_all(blocks, 'gx', split_axis=0, concat_axis=0, tiled=True)  7.28 us
  transfers between devices with their start and end apart: 2, of which 1 were waited for; matrix products, arithmetic and copies ran while one was open for 0% of the time, Pallas kernels for 21%

profile of v1, /device:TPU:0, one launch (start us, length us, event | category | flops | bytes accessed | tf_op | source)
XLA Modules:
  0.0 91.2 jit_solution(12490375001805308611)
XLA Ops:
  0.0 0.0 copy-start.5
  0.0 0.0 copy-start
  0.0 3.7 %shard_map.163 = f32[1152,128]{1,0:T(8,128)S(1)} custom-call(f32[2,24,2,96,128]{4,3,2,1,0:T(8,128)} %bitcast.13, bf16[512,256]{1,0:T(8,128)(2,1)} %constant.22.clone.wz_hbm, bf16[96,192]{1,0:T(8,128)(2,1)} %constant.23.clone.ty_hbm), custom_call_target="tpu_custom_call" | custom-call | bytes 5017600 | tf_op jit(solution)/shard_map/pallas_call | solution.py:70
  3.7 0.0 copy-start.8
  3.7 0.0 copy-start.12
  3.8 24.5 %all_to_all.20.r_ref = f32[16,72,128]{2,1,0:T(8,128)S(1)} all-to-all(f32[16,72,128]{2,1,0:T(8,128)S(1)} %bitcast.9), channel_id=1, replica_groups=mesh['groups'=2,'gx'=16] {'gx'}, dimensions={0} | all-to-all | bytes 1179648 | tf_op jit(solution)/shard_map/all_to_all | solution.py:691
  28.3 0.0 copy-done.5
  28.3 0.0 copy-done
  28.3 3.0 %shard_map.164 = f32[16,72,128]{2,1,0:T(8,128)} custom-call(f32[16,72,128]{2,1,0:T(8,128)S(1)} %all_to_all.20.r_ref, bf16[8,48,48,96]{3,2,1,0:T(8,128)(2,1)S(1)} %bitcast.8, f32[128,128]{1,0:T(8,128)S(1)} %copy-done.5), custom_call_target="tpu_custom_call" | custom-call | bytes 4194304 | tf_op jit(solution)/shard_map/pallas_call | solution.py:70
  31.3 3.6 %all-to-all-start.1 = ((f32[16,72,128]{2,1,0:T(8,128)}), f32[16,72,128]{2,1,0:T(8,128)S(1)}, u32[]{:S(2)}, u32[]{:S(2)}) async-start(f32[16,72,128]{2,1,0:T(8,128)} %shard_map.164), calls=%async_computation.1 | async-start | bytes 1179648 | tf_op jit(solution)/shard_map/all_to_all | solution.py:691
  34.9 0.0 copy-done.8
  34.9 0.0 copy-done.12
  34.9 0.0 copy-start.3
  34.9 0.0 copy-start.6
  34.9 0.0 copy-start.7
  34.9 7.1 %shard_map.165 = (f32[48,2,96,128]{3,2,1,0:T(8,128)}, bf16[2,2048,256]{2,1,0:T(8,128)(2,1)S(1)}) custom-call(f32[48,2,96,128]{3,2,1,0:T(8,128)} %base_hbm.1, f32[48,48]{1,0:T(8,128)S(1)} %copy-done.8, bf16[2,128,256]{2,1,0:T(8,128)(2,1)S(1)} %copy-done.12), custom_call_target="tpu_custom_call" | custom-call | flops 4294967296 | bytes 4858880 | tf_op jit(solution)/shard_map/pallas_call | solution.py:70
  42.0 8.3 %all-to-all-done.1 = f32[16,72,128]{2,1,0:T(8,128)S(1)} async-done(((f32[16,72,128]{2,1,0:T(8,128)}), f32[16,72,128]{2,1,0:T(8,128)S(1)}, u32[]{:S(2)}, u32[]{:S(2)}) %all-to-all-start.1) | async-done | bytes 589856 | tf_op jit(solution)/shard_map/all_to_all | solution.py:691
  50.3 0.0 copy-start.1
  50.3 0.0 copy-done.3
  50.3 0.0 copy-done.6
  50.3 0.0 copy-done.7
  50.3 0.0 copy-start.10
  50.4 5.5 %shard_map.166 = (f32[2,24,2,96,128]{4,3,2,1,0:T(8,128)}, f32[48,48,128]{2,1,0:T(8,128)}, f32[256,128]{1,0:T(8,128)S(1)}) custom-call(f32[1152,128]{1,0:T(8,128)S(1)} %bitcast.10, f32[2,24,2,96,128]{4,3,2,1,0:T(8,128)} %bitcast.14, bf16[96,144]{1,0:T(8,128)(2,1)S(1)} %copy-done.7, bf16[256,512]{1,0:T(8,128)(2,1)S(1)} %copy-done.3, ...), custom_call_target="tpu_custom_call" | custom-call | bytes 7732224 | tf_op jit(solution)/shard_map/pallas_call | solution.py:70
  55.9 12.0 %all_to_all.21.refs_0_ = f32[16,16,128]{2,1,0:T(8,128)S(1)} all-to-all(f32[16,16,128]{2,1,0:T(8,128)S(1)} %bitcast.12), channel_id=1, replica_groups=mesh['groups'=2,'gx'=16] {'gx'}, dimensions={0} | all-to-all | bytes 262144 | tf_op jit(solution)/shard_map/all_to_all | solution.py:691
  67.9 0.0 copy-done.1
  67.9 1.3 %shard_map.167 = f32[16,16,128]{2,1,0:T(8,128)} custom-call(f32[16,16,128]{2,1,0:T(8,128)S(1)} %all_to_all.21.refs_0_, bf16[24,4,48,48]{3,2,1,0:T(8,128)(2,1)S(1)} %copy-done.1), custom_call_target="tpu_custom_call" | custom-call | bytes 573440 | tf_op jit(solution)/shard_map/pallas_call | solution.py:70
  69.2 3.7 %all-to-all-start.3 = ((f32[16,16,128]{2,1,0:T(8,128)}), f32[16,16,128]{2,1,0:T(8,128)S(1)}, u32[]{:S(2)}, u32[]{:S(2)}) async-start(f32[16,16,128]{2,1,0:T(8,128)} %shard_map.167), calls=%async_computation.3 | async-start | bytes 262144 | tf_op jit(solution)/shard_map/all_to_all | solution.py:691
  72.9 0.0 copy-done.10
  72.9 0.0 copy-start.9
  72.9 0.0 copy-start.11
  72.9 0.0 copy-start.13
  73.0 7.5 %shard_map.169.base_hbm = f32[48,2,96,128]{3,2,1,0:T(8,128)} custom-call(f32[48,2,96,128]{3,2,1,0:T(8,128)} %bitcast.15, f32[48,48]{1,0:T(8,128)S(1)} %copy-done.10, f32[48,2,96,128]{3,2,1,0:T(8,128)} %base_hbm.1), custom_call_target="tpu_custom_call" | custom-call | flops 4294967296 | bytes 9446400 | tf_op jit(solution)/shard_map/pallas_call | solution.py:70
  80.4 0.0 copy-start.2
  80.5 0.0 copy-start.4
  80.5 0.0 copy-done.9
  80.5 0.0 copy-done.11
  80.5 0.0 copy-done.13
  80.5 4.3 %shard_map.168 = (f32[144,1024]{1,0:T(8,128)S(1)}, bf16[2,384,384]{2,1,0:T(8,128)(2,1)S(1)}, bf16[2,256,1024]{2,1,0:T(8,128)(2,1)S(1)}) custom-call(f32[48,48,128]{2,1,0:T(8,128)} %get-tuple-element.16.hbm_ref, f32[48,48]{1,0:T(8,128)S(1)} %copy-done.9, bf16[256,128]{1,0:T(8,128)(2,1)S(1)} %copy-done.13, f32[48,48]{1,0:T(8,128)S(1)} %copy-done.10, ...), custom_call_target="tpu_custom_call" | custom-call | flops 2147483648 | bytes 1394688 | tf_op jit(solution)/shard_map/pallas_call | solution.py:70
  84.8 0.0 all-to-all-done.3
  84.9 0.0 copy-done.2
  84.9 0.0 copy-done.4
  84.9 6.2 %shard_map.170 = f32[48,2,96,128]{3,2,1,0:T(8,128)} custom-call(f32[256,128]{1,0:T(8,128)S(1)} %bitcast.11, f32[144,1024]{1,0:T(8,128)S(1)} %get-tuple-element.17.lift_ref, f32[48,2,96,128]{3,2,1,0:T(8,128)} %shard_map.169.base_hbm, bf16[2,384,384]{2,1,0:T(8,128)(2,1)S(1)} %get-tuple-element.19.parts_ref, bf16[2,256,1024]{2,1,0:T(8,128)(2,1)S(1)} %get-tuple-element.20.b_ref, ...), custom_call_target="tpu_custom_call" | custom-call | bytes 7503872 | tf_op jit(solution)/shard_map/pallas_call | solution.py:70
Async XLA Ops:
  0.0 28.3 %copy-start.5 = (f32[128,128]{1,0:T(8,128)S(1)}, f32[128,128]{1,0:T(8,128)}, u32[]{:S(2)}) copy-start(f32[128,128]{1,0:T(8,128)} %constant.24.clone.tv_ref) | copy-start | bytes 196612
  0.0 28.3 %copy-start = (bf16[96,8,48,48]{0,3,2,1:T(8,128)(2,1)S(1)}, bf16[96,8,48,48]{0,3,2,1:T(8,128)(2,1)}, u32[]{:S(2)}) copy-start(bf16[96,8,48,48]{0,3,2,1:T(8,128)(2,1)} %param.18) | copy-start | bytes 10616836
  3.7 31.1 %copy-start.8 = (f32[48,48]{1,0:T(8,128)S(1)}, f32[48,48]{1,0:T(8,128)}, u32[]{:S(2)}) copy-start(f32[48,48]{1,0:T(8,128)} %a_ref.3) | copy-start | bytes 27652
  3.7 31.1 %copy-start.12 = (bf16[2,128,256]{2,1,0:T(8,128)(2,1)S(1)}, bf16[2,128,256]{2,1,0:T(8,128)(2,1)}, u32[]{:S(2)}) copy-start(bf16[2,128,256]{2,1,0:T(8,128)(2,1)} %constant.25.clone.ec_ref) | copy-start | bytes 393220
  31.3 19.1 %all-to-all-start.1 = ((f32[16,72,128]{2,1,0:T(8,128)}), f32[16,72,128]{2,1,0:T(8,128)S(1)}, u32[]{:S(2)}, u32[]{:S(2)}) async-start(f32[16,72,128]{2,1,0:T(8,128)} %shard_map.164), calls=%async_computation.1 | async-start | bytes 1179648 | tf_op jit(solution)/shard_map/all_to_all | solution.py:691
  34.9 15.5 %copy-start.3 = (bf16[256,512]{1,0:T(8,128)(2,1)S(1)}, bf16[256,512]{1,0:T(8,128)(2,1)}, u32[]{:S(2)}) copy-start(bf16[256,512]{1,0:T(8,128)(2,1)} %constant.27.clone.refs_3_) | copy-start | bytes 786436
  34.9 15.5 %copy-start.6 = (bf16[96,192]{1,0:T(8,128)(2,1)S(1)}, bf16[96,192]{1,0:T(8,128)(2,1)}, u32[]{:S(2)}) copy-start(bf16[96,192]{1,0:T(8,128)(2,1)} %constant.28.clone.refs_4_) | copy-start | bytes 110596
  34.9 15.4 %copy-start.7 = (bf16[96,144]{1,0:T(8,128)(2,1)S(1)}, bf16[96,144]{1,0:T(8,128)(2,1)}, u32[]{:S(2)}) copy-start(bf16[96,144]{1,0:T(8,128)(2,1)} %constant.26.clone.refs_2_) | copy-start | bytes 82948
  50.3 17.6 %copy-start.1 = (bf16[24,4,48,48]{3,2,1,0:T(8,128)(2,1)S(1)}, bf16[24,4,48,48]{3,2,1,0:T(8,128)(2,1)}, u32[]{:S(2)}) copy-start(bf16[24,4,48,48]{3,2,1,0:T(8,128)(2,1)} %refs_1_.1) | copy-start | bytes 1327108
  50.3 22.6 %copy-start.10 = (f32[48,48]{1,0:T(8,128)S(1)}, f32[48,48]{1,0:T(8,128)}, u32[]{:S(2)}) copy-start(f32[48,48]{1,0:T(8,128)} %a_ref.5) | copy-start | bytes 27652
  69.2 15.6 %all-to-all-start.3 = ((f32[16,16,128]{2,1,0:T(8,128)}), f32[16,16,128]{2,1,0:T(8,128)S(1)}, u32[]{:S(2)}, u32[]{:S(2)}) async-start(f32[16,16,128]{2,1,0:T(8,128)} %shard_map.167), calls=%async_computation.3 | async-start | bytes 262144 | tf_op jit(solution)/shard_map/all_to_all | solution.py:691
  72.9 7.5 %copy-start.9 = (f32[48,48]{1,0:T(8,128)S(1)}, f32[48,48]{1,0:T(8,128)}, u32[]{:S(2)}) copy-start(f32[48,48]{1,0:T(8,128)} %a_ref.4) | copy-start | bytes 27652
  72.9 7.5 %copy-start.11 = (bf16[2,256,128]{2,1,0:T(8,128)(2,1)S(1)}, bf16[2,256,128]{2,1,0:T(8,128)(2,1)}, u32[]{:S(2)}) copy-start(bf16[2,256,128]{2,1,0:T(8,128)(2,1)} %constant.30.clone.ei_ref) | copy-start | bytes 393220
  72.9 7.5 %copy-start.13 = (bf16[256,128]{1,0:T(8,128)(2,1)S(1)}, bf16[256,128]{1,0:T(8,128)(2,1)}, u32[]{:S(2)}) copy-start(bf16[256,128]{1,0:T(8,128)(2,1)} %constant.29.clone.pz_ref) | copy-start | bytes 196612
  80.4 4.4 %copy-start.2 = (bf16[2,288,256]{2,1,0:T(8,128)(2,1)S(1)}, bf16[2,288,256]{2,1,0:T(8,128)(2,1)}, u32[]{:S(2)}) copy-start(bf16[2,288,256]{2,1,0:T(8,128)(2,1)} %constant.31.clone.yi_ref) | copy-start | bytes 884740
  80.5 4.4 %copy-start.4 = (bf16[256,256]{1,0:T(8,128)(2,1)S(1)}, bf16[256,256]{1,0:T(8,128)(2,1)}, u32[]{:S(2)}) copy-start(bf16[256,256]{1,0:T(8,128)(2,1)} %constant.32.clone.up_ref) | copy-start | bytes 393220
